TPU v7x, 128 devices: a whole 4x4x4 slice. The times are simulated.
128 devices in a mesh: band: 64 (over y, z, x_hi, core), grid: 2 (over x_lo).
Axes of the slice: x: 4 (x_hi: 2, x_lo: 2; x = x_hi * 2 + x_lo), y: 4, z: 4, core: 2. Of those that a mesh axis runs over, the one named last changes fastest.
Arguments:
- bands: float32 [128, 72, 5184], P('band', 'grid'), may hold values from -2.4 to 2.4
Outputs:
- exchange_terms: float32 [128, 72, 5184], P('band', 'grid')
All inputs are finite; a program needn't handle non-finite values.
Results may differ from a plain program's by a relative error of at most 0.0001.
Values sent between devices are 32-bit elements; how exact they have to be, the bound alone decides.
A program may use at most 128 MiB of HBM per device.

v0:
```python
import math
import jax
import jax.numpy as jnp
from jax import lax
from jax.sharding import PartitionSpec as P

GRID = 72
STEPS = 3
spacing = 0.5167


def shifted(value, axis, steps):
    count = lax.axis_size(axis)
    pairs = [(source, (source + steps) % count) for source in range(count)]
    return lax.ppermute(value, axis, pairs)


def split_up(array, dim, devices):
    before, after = (array.shape[:dim], array.shape[dim + 1 :])
    return jnp.moveaxis(array.reshape(*before, devices, -1, *after), dim, 0)


def sent_and_summed(array, axis, dim):
    devices = lax.axis_size(axis)
    blocks = lax.all_to_all(split_up(array, dim, devices), axis, 0, 0, tiled=True)
    return jnp.sum(blocks, axis=0)


def tables(count):
    index = jnp.arange(count, dtype=jnp.int32)
    half = count // 2
    freq = jnp.where(index <= half, index, index - half)
    phase = (freq[:, None] * index[None, :] % count).astype(jnp.float32) * (2.0 * math.pi / count)
    table = jnp.where(index[:, None] <= half, jnp.cos(phase), jnp.sin(phase))
    weight = jnp.where((index == 0) | (index == half), 1.0, 2.0).astype(jnp.float32)
    square = freq.astype(jnp.float32) ** 2
    factor = (2.0 * math.pi / (count * spacing)) ** 2
    ksq = factor * (square[:, None, None] + square[None, :, None] + square[None, None, :])
    safe = jnp.where(ksq > 0, ksq, 1.0)
    coulomb = jnp.where(ksq > 0, 4.0 * math.pi / safe, 0.0)
    weights = weight[:, None, None] * weight[None, :, None] * weight[None, None, :]
    kernel = coulomb * weights / float(count**3)
    return (table, kernel.reshape(count, count * count))


def forward_axis(values, table):
    return jnp.einsum("pmc,kc->pkm", values, table, precision=lax.Precision.HIGHEST)


def inverse_axis(values, table):
    return jnp.einsum("pmk,kr->prm", values, table, precision=lax.Precision.HIGHEST)


def coulomb_filter(density, table, kernel):
    count = table.shape[0]
    pairs = density.shape[0]
    work = forward_axis(density.reshape(pairs, count * count, count), table)
    work = forward_axis(work.reshape(pairs, count * count, count), table)
    work = forward_axis(work.reshape(pairs, count * count, count), table)
    work = work * kernel[None]
    work = inverse_axis(work.reshape(pairs, count * count, count), table)
    work = inverse_axis(work.reshape(pairs, count * count, count), table)
    work = inverse_axis(work.reshape(pairs, count * count, count), table)
    return work


def pair_terms(home, visit, table, kernel):
    home_count = home.shape[0]
    visit_count = visit.shape[0]
    count = home.shape[1]
    density = (home[:, None] * visit[None]).reshape(home_count * visit_count, count, home.shape[2])
    potential = coulomb_filter(density, table, kernel).reshape(
        home_count, visit_count, count, home.shape[2]
    )
    home_part = -jnp.sum(potential * visit[None], axis=1)
    partner = -jnp.sum(potential * home[:, None], axis=0)
    return (home_part, partner)


def local(bands):
    table, kernel = tables(GRID)
    whole = lax.all_gather(bands, "grid", axis=1, tiled=True)
    share = whole.shape[0] // lax.axis_size("grid")
    first = lax.axis_index("grid") * share
    visit = lax.dynamic_slice_in_dim(whole, first, share, 0)
    home_total = jnp.zeros_like(whole)
    carried = jnp.zeros_like(visit)
    for step in range(STEPS):
        visit = shifted(visit, "band", 1)
        home_part, partner = pair_terms(whole, visit, table, kernel)
        home_total = home_total + home_part
        carried = carried + partner
        if step + 1 < STEPS:
            carried = shifted(carried, "band", 1)
    returned = shifted(carried, "band", -STEPS)
    own_rows = lax.dynamic_slice_in_dim(home_total, first, share, 0) + returned
    home_total = lax.dynamic_update_slice_in_dim(home_total, own_rows, first, 0)
    return sent_and_summed(home_total, "grid", 1)


def solution(mesh):
    return jax.shard_map(
        local,
        mesh=mesh,
        in_specs=(P("band", "grid", None),),
        out_specs=P("band", "grid", None),
        check_vma=False,
    )
```

profile of v0, /device:TPU:4, one launch (start us, length us, event | category | flops | bytes accessed | tf_op | source)
XLA Modules:
  0.0 540.2 jit_solution(13337431884350394181)
XLA Ops:
  7.3 49.8 %all-gather.2.cloned.1.call-done = f32[2,72,5184]{2,0,1:T(2,128)} async-done(((f32[2,36,5184]{2,0,1:T(2,128)}), f32[2,72,5184]{2,0,1:T(2,128)}) %all-gather.2.cloned.1.call-update) | async-done | bytes 2986000 | tf_op jit(solution)/shard_map/all_gather | solution.py:82
  60.3 20.7 %collective-permute-done = f32[1,72,5184]{2,0,1:T(1,128)S(1)} collective-permute-done((f32[1,72,5184]{2,0,1:T(1,128)S(1)}, f32[1,72,5184]{2,0,1:T(1,128)S(1)}, u32[]{:S(2)}, u32[]{:S(2)}) %collective-permute-start) | collective-permute-done | bytes 1493024 | tf_op jit(solution)/shard_map/ppermute | solution.py:15
  82.3 20.6 %collective-permute-done.1 = f32[1,72,5184]{2,0,1:T(1,128)} collective-permute-done((f32[1,72,5184]{2,0,1:T(1,128)S(1)}, f32[1,72,5184]{2,0,1:T(1,128)}, u32[]{:S(2)}, u32[]{:S(2)}) %collective-permute-start.1) | collective-permute-done | bytes 1493024 | tf_op jit(solution)/shard_map/ppermute | solution.py:15
  113.3 10.6 %collective-permute-done.2 = f32[1,72,5184]{2,0,1:T(1,128)} collective-permute-done((f32[1,72,5184]{2,0,1:T(1,128)}, f32[1,72,5184]{2,0,1:T(1,128)}, u32[]{:S(2)}, u32[]{:S(2)}) %collective-permute-start.2) | collective-permute-done | bytes 1493024 | tf_op jit(solution)/shard_map/ppermute | solution.py:15
  135.5 9.4 %convolution_bitcast_fusion.14 = f32[2,72,5184]{2,1,0:T(8,128)} fusion(f32[2,5184,72]{2,1,0:T(8,128)} %reshape_reshape.9, s32[72]{0:T(128)S(1)} %add_select_fusion.1, pred[72]{0:T(512)(128)(4,1)S(1)} %iota_compare_fusion), kind=kOutput, calls=%fused_computation.20 | convolution fusion | flops 645024384 | bytes 5972328 | tf_op jit(solution)/shard_map/pmc,kc->pkm/dot_general | solution.py:47
  150.8 9.4 %convolution_bitcast_fusion.13 = f32[2,72,5184]{2,1,0:T(8,128)} fusion(f32[2,5184,72]{2,1,0:T(8,128)} %reshape.283, s32[72]{0:T(128)S(1)} %add_select_fusion.1, pred[72]{0:T(512)(128)(4,1)S(1)} %iota_compare_fusion), kind=kOutput, calls=%fused_computation.19 | convolution fusion | flops 645024384 | bytes 5972328 | tf_op jit(solution)/shard_map/pmc,kc->pkm/dot_general | solution.py:47
  166.2 9.4 %fusion = f32[2,72,5184]{2,1,0:T(8,128)} fusion(f32[2,5184,72]{2,1,0:T(8,128)} %reshape.284, f32[72,5184]{1,0:T(8,128)S(1)} %fusion.5, s32[72]{0:T(128)S(1)} %add_select_fusion.1, pred[72]{0:T(512)(128)(4,1)S(1)} %iota_compare_fusion), kind=kOutput, calls=%fused_computation.3 | convolution fusion | flops 645770880 | bytes 7465320 | tf_op jit(solution)/shard_map/pmc,kc->pkm/dot_general | solution.py:47
  181.5 9.7 %convolution_bitcast_fusion.12 = f32[2,72,5184]{2,1,0:T(8,128)} fusion(f32[2,5184,72]{2,1,0:T(8,128)} %reshape.285, s32[72]{0:T(128)S(1)} %add_select_fusion.1, pred[72]{0:T(512)(128)(4,1)S(1)} %iota_compare_fusion), kind=kOutput, calls=%fused_computation.18 | convolution fusion | flops 645024384 | bytes 5972328 | tf_op jit(solution)/shard_map/pmk,kr->prm/dot_general | solution.py:51
  197.4 9.7 %convolution_bitcast_fusion.11 = f32[2,72,5184]{2,1,0:T(8,128)} fusion(f32[2,5184,72]{2,1,0:T(8,128)} %reshape.286, s32[72]{0:T(128)S(1)} %add_select_fusion.1, pred[72]{0:T(512)(128)(4,1)S(1)} %iota_compare_fusion), kind=kOutput, calls=%fused_computation.17 | convolution fusion | flops 645024384 | bytes 5972328 | tf_op jit(solution)/shard_map/pmk,kr->prm/dot_general | solution.py:51
  213.0 9.7 %convolution_bitcast_fusion.10 = f32[2,72,5184]{2,1,0:T(8,128)} fusion(f32[2,5184,72]{2,1,0:T(8,128)} %reshape.287, s32[72]{0:T(128)S(1)} %add_select_fusion.1, pred[72]{0:T(512)(128)(4,1)S(1)} %iota_compare_fusion), kind=kOutput, calls=%fused_computation.16 | convolution fusion | flops 645024384 | bytes 5972328 | tf_op jit(solution)/shard_map/pmk,kr->prm/dot_general | solution.py:51
  243.8 9.3 %convolution_bitcast_fusion.8 = f32[2,72,5184]{2,1,0:T(8,128)} fusion(f32[2,5184,72]{2,1,0:T(8,128)} %reshape.288, s32[72]{0:T(128)S(1)} %add_select_fusion.1, pred[72]{0:T(512)(128)(4,1)S(1)} %iota_compare_fusion), kind=kOutput, calls=%fused_computation.14 | convolution fusion | flops 645024384 | bytes 5972328 | tf_op jit(solution)/shard_map/pmc,kc->pkm/dot_general | solution.py:47
  274.3 9.6 %convolution_bitcast_fusion.7 = f32[2,72,5184]{2,1,0:T(8,128)} fusion(f32[2,5184,72]{2,1,0:T(8,128)} %reshape.290, s32[72]{0:T(128)S(1)} %add_select_fusion.1, pred[72]{0:T(512)(128)(4,1)S(1)} %iota_compare_fusion), kind=kOutput, calls=%fused_computation.13 | convolution fusion | flops 645024384 | bytes 5972328 | tf_op jit(solution)/shard_map/pmk,kr->prm/dot_general | solution.py:51
  290.1 9.6 %convolution_bitcast_fusion.6 = f32[2,72,5184]{2,1,0:T(8,128)} fusion(f32[2,5184,72]{2,1,0:T(8,128)} %reshape.291, s32[72]{0:T(128)S(1)} %add_select_fusion.1, pred[72]{0:T(512)(128)(4,1)S(1)} %iota_compare_fusion), kind=kOutput, calls=%fused_computation.12 | convolution fusion | flops 645024384 | bytes 5972328 | tf_op jit(solution)/shard_map/pmk,kr->prm/dot_general | solution.py:51
  305.5 9.6 %convolution_bitcast_fusion.5 = f32[2,72,5184]{2,1,0:T(8,128)} fusion(f32[2,5184,72]{2,1,0:T(8,128)} %reshape.292, s32[72]{0:T(128)S(1)} %add_select_fusion.1, pred[72]{0:T(512)(128)(4,1)S(1)} %iota_compare_fusion), kind=kOutput, calls=%fused_computation.11 | convolution fusion | flops 645024384 | bytes 5972328 | tf_op jit(solution)/shard_map/pmk,kr->prm/dot_general | solution.py:51
  321.1 9.4 %convolution_bitcast_fusion.4 = f32[2,72,5184]{2,1,0:T(8,128)} fusion(f32[2,5184,72]{2,1,0:T(8,128)} %reshape_reshape.11, s32[72]{0:T(128)S(1)} %add_select_fusion.1, pred[72]{0:T(512)(128)(4,1)S(1)} %iota_compare_fusion), kind=kOutput, calls=%fused_computation.10 | convolution fusion | flops 645024384 | bytes 5972328 | tf_op jit(solution)/shard_map/pmc,kc->pkm/dot_general | solution.py:47
  336.3 9.4 %convolution_bitcast_fusion.3 = f32[2,72,5184]{2,1,0:T(8,128)} fusion(f32[2,5184,72]{2,1,0:T(8,128)} %reshape.293, s32[72]{0:T(128)S(1)} %add_select_fusion.1, pred[72]{0:T(512)(128)(4,1)S(1)} %iota_compare_fusion), kind=kOutput, calls=%fused_computation.9 | convolution fusion | flops 645024384 | bytes 5972328 | tf_op jit(solution)/shard_map/pmc,kc->pkm/dot_general | solution.py:47
  351.8 9.4 %fusion.2 = f32[2,72,5184]{2,1,0:T(8,128)} fusion(f32[2,5184,72]{2,1,0:T(8,128)} %reshape.294, f32[72,5184]{1,0:T(8,128)S(1)} %fusion.5, s32[72]{0:T(128)S(1)} %add_select_fusion.1, pred[72]{0:T(512)(128)(4,1)S(1)} %iota_compare_fusion), kind=kOutput, calls=%fused_computation.5 | convolution fusion | flops 645770880 | bytes 7465320 | tf_op jit(solution)/shard_map/pmc,kc->pkm/dot_general | solution.py:47
  379.6 9.7 %convolution_bitcast_fusion.1 = f32[2,72,5184]{2,1,0:T(8,128)} fusion(f32[2,5184,72]{2,1,0:T(8,128)} %reshape.296, s32[72]{0:T(128)S(1)} %add_select_fusion.1, pred[72]{0:T(512)(128)(4,1)S(1)} %iota_compare_fusion), kind=kOutput, calls=%fused_computation.7 | convolution fusion | flops 645024384 | bytes 5972328 | tf_op jit(solution)/shard_map/pmk,kr->prm/dot_general | solution.py:51
  395.5 13.0 %multiply_reduce_fusion = (f32[72,5184]{1,0:T(8,128)S(1)}, f32[72,5184]{1,0:T(8,128)S(1)}, f32[72,5184]{1,0:T(8,128)S(1)}, f32[2,72,5184]{2,1,0:T(8,128)S(1)}) fusion(f32[2,72,5184]{2,0,1:T(2,128)S(1)} %copy-done.1, f32[2,72,5184]{2,1,0:T(8,128)} %convolution_bitcast_fusion.10, f32[2,72,5184]{2,1,0:T(8,128)} %convolution_bitcast_fusion.5, ...), kind=kOutput, calls=%fused_computation.21 | convolution fusion | flops 654355584 | bytes 23888232 | tf_op jit(solution)/shard_map/pmk,kr->prm/dot_general | solution.py:51
  408.7 20.7 %collective-permute-done.3 = f32[1,72,5184]{2,1,0:T(8,128)S(1)} collective-permute-done((f32[1,72,5184]{2,1,0:T(8,128)S(1)}, f32[1,72,5184]{2,1,0:T(8,128)S(1)}, u32[]{:S(2)}, u32[]{:S(2)}) %collective-permute-start.3) | collective-permute-done | bytes 1493024 | tf_op jit(solution)/shard_map/ppermute | solution.py:15
  430.2 20.0 %collective-permute-done.4 = f32[1,72,5184]{2,1,0:T(8,128)S(1)} collective-permute-done((f32[1,72,5184]{2,1,0:T(8,128)S(1)}, f32[1,72,5184]{2,1,0:T(8,128)S(1)}, u32[]{:S(2)}, u32[]{:S(2)}) %collective-permute-start.4) | collective-permute-done | bytes 1493024 | tf_op jit(solution)/shard_map/ppermute | solution.py:15
  450.4 18.3 %collective-permute-start.5 = (f32[1,72,5184]{2,1,0:T(8,128)S(1)}, f32[1,72,5184]{2,1,0:T(8,128)S(1)}, u32[]{:S(2)}, u32[]{:S(2)}) collective-permute-start(f32[1,72,5184]{2,1,0:T(8,128)S(1)} %bitcast_add_fusion), channel_id=1, source_target_pairs={{0,122},{2,124},{4,126},{6,0},{8,2},{10,4},{12,6},{14,8},{16,10},{... | collective-permute-start | bytes 4478984 | tf_op jit(solution)/shard_map/ppermute | solution.py:15
  468.7 22.2 %collective-permute-done.5 = f32[1,72,5184]{2,1,0:T(8,128)S(1)} collective-permute-done((f32[1,72,5184]{2,1,0:T(8,128)S(1)}, f32[1,72,5184]{2,1,0:T(8,128)S(1)}, u32[]{:S(2)}, u32[]{:S(2)}) %collective-permute-start.5) | collective-permute-done | bytes 1493024 | tf_op jit(solution)/shard_map/ppermute | solution.py:15
  492.8 36.3 %all_to_all.5 = f32[2,2,36,5184]{3,1,2,0:T(2,128)S(1)} all-to-all(f32[2,2,36,5184]{3,1,2,0:T(2,128)S(1)} %bitcast.126), channel_id=1, replica_groups=mesh['band'=64,'grid'=2] {'grid'}, dimensions={0} | all-to-all | bytes 5971968 | tf_op jit(solution)/shard_map/all_to_all | solution.py:25
  (68 shorter events, 160.6 us)
Async XLA Ops:
  6.5 50.6 %all-gather.2.cloned.1.call-start = ((), (), s32[]{:S(2)}) async-start(), calls=%async_computation.1 | async-start | bytes 4534272 | tf_op jit(solution)/shard_map/all_gather | solution.py:82
  60.2 20.8 %collective-permute-start = (f32[1,72,5184]{2,0,1:T(1,128)S(1)}, f32[1,72,5184]{2,0,1:T(1,128)S(1)}, u32[]{:S(2)}, u32[]{:S(2)}) collective-permute-start(f32[1,72,5184]{2,0,1:T(1,128)S(1)} %constant_dynamic-slice_fusion), channel_id=1, source_target_pairs={{0,2},{2,4},{4,6},{6,8},{8,10},{10,12},{12,14},{14,16},{16,18},{18... | collective-permute-start | bytes 4478984 | tf_op jit(solution)/shard_map/ppermute | solution.py:15
  81.0 1.1 copy-start.5
  82.1 20.8 %collective-permute-start.1 = (f32[1,72,5184]{2,0,1:T(1,128)S(1)}, f32[1,72,5184]{2,0,1:T(1,128)}, u32[]{:S(2)}, u32[]{:S(2)}) collective-permute-start(f32[1,72,5184]{2,0,1:T(1,128)S(1)} %collective-permute-done), channel_id=1, source_target_pairs={{0,2},{2,4},{4,6},{6,8},{8,10},{10,12},{12,14},{14,16},{16,18},{18... | collective-permute-start | bytes 4478984 | tf_op jit(solution)/shard_map/ppermute | solution.py:15
  102.9 21.0 %collective-permute-start.2 = (f32[1,72,5184]{2,0,1:T(1,128)}, f32[1,72,5184]{2,0,1:T(1,128)}, u32[]{:S(2)}, u32[]{:S(2)}) collective-permute-start(f32[1,72,5184]{2,0,1:T(1,128)} %collective-permute-done.1), channel_id=1, source_target_pairs={{0,2},{2,4},{4,6},{6,8},{8,10},{10,12},{12,14},{14,16},{16,18},{18... | collective-permute-start | bytes 4478984 | tf_op jit(solution)/shard_map/ppermute | solution.py:15
  108.6 2.5 copy-start.6
  111.2 14.3 %copy-start.2 = (f32[1,72,5184]{2,1,0:T(8,128)}, f32[1,72,5184]{2,1,0:T(8,128)S(1)}, u32[]{:S(2)}) copy-start(f32[1,72,5184]{2,1,0:T(8,128)S(1)} %copy.143) | copy-start | bytes 4478980
  111.2 14.3 %copy-start = (f32[2,72,5184]{2,0,1:T(2,128)S(1)}, f32[2,72,5184]{2,0,1:T(2,128)}, u32[]{:S(2)}) copy-start(f32[2,72,5184]{2,0,1:T(2,128)} %all-gather.2.cloned.1.call-done) | copy-start | bytes 8957956
  113.3 16.3 %copy-start.3 = (f32[1,72,5184]{2,1,0:T(8,128)}, f32[1,72,5184]{2,1,0:T(8,128)S(1)}, u32[]{:S(2)}) copy-start(f32[1,72,5184]{2,1,0:T(8,128)S(1)} %copy.142) | copy-start | bytes 4478980
  125.4 4.1 copy-start.4
  389.3 6.1 %copy-start.1 = (f32[2,72,5184]{2,0,1:T(2,128)S(1)}, f32[2,72,5184]{2,0,1:T(2,128)}, u32[]{:S(2)}) copy-start(f32[2,72,5184]{2,0,1:T(2,128)} %all-gather.2.cloned.1.call-done) | copy-start | bytes 8957956
  408.6 20.8 %collective-permute-start.3 = (f32[1,72,5184]{2,1,0:T(8,128)S(1)}, f32[1,72,5184]{2,1,0:T(8,128)S(1)}, u32[]{:S(2)}, u32[]{:S(2)}) collective-permute-start(f32[1,72,5184]{2,1,0:T(8,128)S(1)} %negate_bitcast_fusion), channel_id=1, source_target_pairs={{0,2},{2,4},{4,6},{6,8},{8,10},{10,12},{12,14},{14,16},{16,18},{18... | collective-permute-start | bytes 4478984 | tf_op jit(solution)/shard_map/ppermute | solution.py:15
  429.5 20.8 %collective-permute-start.4 = (f32[1,72,5184]{2,1,0:T(8,128)S(1)}, f32[1,72,5184]{2,1,0:T(8,128)S(1)}, u32[]{:S(2)}, u32[]{:S(2)}) collective-permute-start(f32[1,72,5184]{2,1,0:T(8,128)S(1)} %bitcast_add_fusion.1), channel_id=1, source_target_pairs={{0,2},{2,4},{4,6},{6,8},{8,10},{10,12},{12,14},{14,16},{16,18},{18... | collective-permute-start | bytes 4478984 | tf_op jit(solution)/shard_map/ppermute | solution.py:15
  450.4 40.5 %collective-permute-start.5 = (f32[1,72,5184]{2,1,0:T(8,128)S(1)}, f32[1,72,5184]{2,1,0:T(8,128)S(1)}, u32[]{:S(2)}, u32[]{:S(2)}) collective-permute-start(f32[1,72,5184]{2,1,0:T(8,128)S(1)} %bitcast_add_fusion), channel_id=1, source_target_pairs={{0,122},{2,124},{4,126},{6,0},{8,2},{10,4},{12,6},{14,8},{16,10},{... | collective-permute-start | bytes 4478984 | tf_op jit(solution)/shard_map/ppermute | solution.py:15
Sparse Core Ops, SparseCore 0:
  9.0 48.0 all-gather.1
where the time goes:
time: 548 us; the launch traced here: 540 us
  matrix products  173 us (32%)
  waiting for transfers between devices  165 us (30%)
  local copies, waits for them, and re-layouts  121 us (22%)
  blocking collectives  36.3 us (7%)
  starting transfers between devices  19.2 us (4%)
  between operations  13.8 us (3%)
  other arithmetic  11.4 us (2%)
    ppermute x6, waiting for transfers between devices, shifted(): return lax.ppermute(value, axis, pairs)  115 us
    dot_general x9, matrix products, inverse_axis(): jnp.einsum('pmk,kr->prm', values, table, precision=lax.Precision.HIGHEST)  88.6 us
    dot_general x9, matrix products, forward_axis(): jnp.einsum('pmc,kc->pkm', values, table, precision=lax.Precision.HIGHEST)  84.5 us
    reshape x9, local copies, waits for them, and re-layouts, coulomb_filter(): work = inverse_axis(work.reshape(pairs, count * count, count), table)  52.3 us
    all_gather x1, waiting for transfers between devices, local(): whole = lax.all_gather(bands, 'grid', axis=1, tiled=True)  49.8 us
    all_to_all x1, blocking collectives, sent_and_summed(): lax.all_to_all(split_up(array, dim, devices), axis, 0, 0, tiled=True)  36.3 us
    reshape x6, local copies, waits for them, and re-layouts, coulomb_filter(): work = forward_axis(work.reshape(pairs, count * count, count), table)  35.6 us
    ppermute x6, starting transfers between devices, shifted(): return lax.ppermute(value, axis, pairs)  19.2 us
  transfers between devices with their start and end apart: 7, of which 7 were waited for; matrix products, arithmetic and copies ran while one was open for 2% of the time, Pallas kernels for 0%

commit v1 on v0

--- a/solution.py
+++ b/solution.py
@@ -79,7 +79,15 @@
 
 def local(bands):
     table, kernel = tables(GRID)
-    whole = lax.all_gather(bands, "grid", axis=1, tiled=True)
+    whole = jnp.concatenate(
+        lax.all_to_all(
+            jnp.stack([bands for _ in range(lax.axis_size("grid"))], 0),
+            axis_name="grid",
+            split_axis=0,
+            concat_axis=0,
+        ),
+        1,
+    )
     share = whole.shape[0] // lax.axis_size("grid")
     first = lax.axis_index("grid") * share
     visit = lax.dynamic_slice_in_dim(whole, first, share, 0)

time: 548 us -> 504 us (0.920)
  waiting for transfers between devices: 165 us -> 107 us
  other arithmetic: 11.4 us -> 32.9 us
  between operations: 13.8 us -> 0.42 us
  local copies, waits for them, and re-layouts: 121 us -> 130 us
    all_gather x1 -> x0, waiting for transfers between devices: 49.8 us -> none  [local(): whole = lax.all_gather(bands, 'grid', axis=1, tiled=True)]
    ppermute x6, waiting for transfers between devices: 115 us -> 71.8 us  [shifted(): return lax.ppermute(value, axis, pairs)]
    all_to_all x0 -> x1, waiting for transfers between devices: none -> 34.8 us  [local(): lax.all_to_all(jnp.stack([bands for _ in range(lax.axis_size('grid'))], 0...]
    ppermute x0 -> x3, other arithmetic: none -> 18.4 us  [shifted(): return lax.ppermute(value, axis, pairs)]
    another operation x3 -> x1, local copies, waits for them, and re-layouts: 18 us -> 5.92 us  [pair_terms(): home[:, None] * visit[None]]
    mul x0 -> x3, local copies, waits for them, and re-layouts: none -> 11.3 us  [pair_terms(): home[:, None] * visit[None]]
    ppermute x6, starting transfers between devices: 19.2 us -> 12.8 us  [shifted(): return lax.ppermute(value, axis, pairs)]
  transfers between devices with their start and end apart: 7 -> 7, of which waited for: 7 -> 4; matrix products, arithmetic and copies ran while one was open for 2% -> 28% of each run, Pallas kernels for 0% -> 0%
where the time goes in v1:
time: 504 us; the launch traced here: 499 us
  matrix products  178 us (35%)
  local copies, waits for them, and re-layouts  130 us (26%)
  waiting for transfers between devices  107 us (21%)
  blocking collectives  34.3 us (7%)
  other arithmetic  32.9 us (7%)
  starting transfers between devices  16.7 us (3%)
    dot_general x9, matrix products, inverse_axis(): jnp.einsum('pmk,kr->prm', values, table, precision=lax.Precision.HIGHEST)  89.2 us
    dot_general x9, matrix products, forward_axis(): jnp.einsum('pmc,kc->pkm', values, table, precision=lax.Precision.HIGHEST)  88.7 us
    ppermute x6, waiting for transfers between devices, shifted(): return lax.ppermute(value, axis, pairs)  71.8 us
    reshape x9, local copies, waits for them, and re-layouts, coulomb_filter(): work = inverse_axis(work.reshape(pairs, count * count, count), table)  53.4 us
    reshape x6, local copies, waits for them, and re-layouts, coulomb_filter(): work = forward_axis(work.reshape(pairs, count * count, count), table)  35.2 us
    all_to_all x1, waiting for transfers between devices, local(): lax.all_to_all(jnp.stack([bands for _ in range(lax.axis_size('grid'))], 0...  34.8 us
    all_to_all x1, blocking collectives, sent_and_summed(): lax.all_to_all(split_up(array, dim, devices), axis, 0, 0, tiled=True)  34.3 us
    ppermute x3, other arithmetic, shifted(): return lax.ppermute(value, axis, pairs)  18.4 us
  transfers between devices with their start and end apart: 7, of which 4 were waited for; matrix products, arithmetic and copies ran while one was open for 28% of the time, Pallas kernels for 0%

profile of v1, /device:TPU:4, one launch (start us, length us, event | category | flops | bytes accessed | tf_op | source)
XLA Modules:
  0.0 498.5 jit_solution(2676811077681852908)
XLA Ops:
  9.0 34.8 %all-to-all-done = f32[2,2,36,5184]{3,1,2,0:T(2,128)S(1)} async-done(((f32[2,2,36,5184]{3,1,2,0:T(2,128)}), f32[2,2,36,5184]{3,1,2,0:T(2,128)S(1)}, u32[]{:S(2)}, u32[]{:S(2)}) %all-to-all-start) | async-done | bytes 2986016 | tf_op jit(solution)/shard_map/all_to_all | solution.py:83
  78.2 10.4 %convolution_bitcast_fusion.14 = f32[2,72,5184]{2,1,0:T(8,128)} fusion(f32[2,5184,72]{2,1,0:T(8,128)} %broadcast_in_dim_reshape.2, f32[5184,72]{1,0:T(8,128)} %mul.373, s32[72]{0:T(128)S(1)} %add_select_fusion.1, pred[72]{0:T(512)(128)(4,1)S(1)} %iota_compare_fusion), kind=kOutput, calls=%fused_computation.20 | convolution fusion | flops 645770880 | bytes 7465320 | tf_op jit(solution)/shard_map/pmc,kc->pkm/dot_general | solution.py:47
  94.5 9.4 %convolution_bitcast_fusion.13 = f32[2,72,5184]{2,1,0:T(8,128)} fusion(f32[2,5184,72]{2,1,0:T(8,128)} %reshape.306, s32[72]{0:T(128)S(1)} %add_select_fusion.1, pred[72]{0:T(512)(128)(4,1)S(1)} %iota_compare_fusion), kind=kOutput, calls=%fused_computation.19 | convolution fusion | flops 645024384 | bytes 5972328 | tf_op jit(solution)/shard_map/pmc,kc->pkm/dot_general | solution.py:47
  111.9 9.9 %fusion = f32[2,72,5184]{2,1,0:T(8,128)} fusion(f32[2,5184,72]{2,1,0:T(8,128)} %reshape.307, f32[72,5184]{1,0:T(8,128)} %fusion.11, s32[72]{0:T(128)S(1)} %add_select_fusion.1, pred[72]{0:T(512)(128)(4,1)S(1)} %iota_compare_fusion), kind=kOutput, calls=%fused_computation.3 | convolution fusion | flops 645770880 | bytes 7465320 | tf_op jit(solution)/shard_map/pmc,kc->pkm/dot_general | solution.py:47
  127.7 9.7 %convolution_bitcast_fusion.12 = f32[2,72,5184]{2,1,0:T(8,128)} fusion(f32[2,5184,72]{2,1,0:T(8,128)} %reshape.308, s32[72]{0:T(128)S(1)} %add_select_fusion.1, pred[72]{0:T(512)(128)(4,1)S(1)} %iota_compare_fusion), kind=kOutput, calls=%fused_computation.18 | convolution fusion | flops 645024384 | bytes 5972328 | tf_op jit(solution)/shard_map/pmk,kr->prm/dot_general | solution.py:51
  143.3 9.7 %convolution_bitcast_fusion.11 = f32[2,72,5184]{2,1,0:T(8,128)} fusion(f32[2,5184,72]{2,1,0:T(8,128)} %reshape.309, s32[72]{0:T(128)S(1)} %add_select_fusion.1, pred[72]{0:T(512)(128)(4,1)S(1)} %iota_compare_fusion), kind=kOutput, calls=%fused_computation.17 | convolution fusion | flops 645024384 | bytes 5972328 | tf_op jit(solution)/shard_map/pmk,kr->prm/dot_general | solution.py:51
  161.8 9.7 %convolution_bitcast_fusion.10 = f32[2,72,5184]{2,1,0:T(8,128)} fusion(f32[2,5184,72]{2,1,0:T(8,128)} %reshape.310, s32[72]{0:T(128)S(1)} %add_select_fusion.1, pred[72]{0:T(512)(128)(4,1)S(1)} %iota_compare_fusion), kind=kOutput, calls=%fused_computation.16 | convolution fusion | flops 645024384 | bytes 5972328 | tf_op jit(solution)/shard_map/pmk,kr->prm/dot_general | solution.py:51
  181.3 10.3 %convolution_bitcast_fusion.9 = f32[2,72,5184]{2,1,0:T(8,128)} fusion(f32[2,5184,72]{2,1,0:T(8,128)} %broadcast_in_dim_reshape.2, f32[5184,72]{1,0:T(8,128)} %mul.393, s32[72]{0:T(128)S(1)} %add_select_fusion.1, pred[72]{0:T(512)(128)(4,1)S(1)} %iota_compare_fusion), kind=kOutput, calls=%fused_computation.15 | convolution fusion | flops 645770880 | bytes 7465320 | tf_op jit(solution)/shard_map/pmc,kc->pkm/dot_general | solution.py:47
  197.5 9.3 %convolution_bitcast_fusion.8 = f32[2,72,5184]{2,1,0:T(8,128)} fusion(f32[2,5184,72]{2,1,0:T(8,128)} %reshape.311, s32[72]{0:T(128)S(1)} %add_select_fusion.1, pred[72]{0:T(512)(128)(4,1)S(1)} %iota_compare_fusion), kind=kOutput, calls=%fused_computation.14 | convolution fusion | flops 645024384 | bytes 5972328 | tf_op jit(solution)/shard_map/pmc,kc->pkm/dot_general | solution.py:47
  213.2 9.8 %fusion.1 = f32[2,72,5184]{2,1,0:T(8,128)} fusion(f32[2,5184,72]{2,1,0:T(8,128)} %reshape.312, f32[72,5184]{1,0:T(8,128)} %fusion.11, s32[72]{0:T(128)S(1)} %add_select_fusion.1, pred[72]{0:T(512)(128)(4,1)S(1)} %iota_compare_fusion), kind=kOutput, calls=%fused_computation.4 | convolution fusion | flops 645770880 | bytes 7465320 | tf_op jit(solution)/shard_map/pmc,kc->pkm/dot_general | solution.py:47
  228.8 9.6 %convolution_bitcast_fusion.7 = f32[2,72,5184]{2,1,0:T(8,128)} fusion(f32[2,5184,72]{2,1,0:T(8,128)} %reshape.313, s32[72]{0:T(128)S(1)} %add_select_fusion.1, pred[72]{0:T(512)(128)(4,1)S(1)} %iota_compare_fusion), kind=kOutput, calls=%fused_computation.13 | convolution fusion | flops 645024384 | bytes 5972328 | tf_op jit(solution)/shard_map/pmk,kr->prm/dot_general | solution.py:51
  244.3 9.6 %convolution_bitcast_fusion.6 = f32[2,72,5184]{2,1,0:T(8,128)} fusion(f32[2,5184,72]{2,1,0:T(8,128)} %reshape.314, s32[72]{0:T(128)S(1)} %add_select_fusion.1, pred[72]{0:T(512)(128)(4,1)S(1)} %iota_compare_fusion), kind=kOutput, calls=%fused_computation.12 | convolution fusion | flops 645024384 | bytes 5972328 | tf_op jit(solution)/shard_map/pmk,kr->prm/dot_general | solution.py:51
  262.5 9.6 %convolution_bitcast_fusion.5 = f32[2,72,5184]{2,1,0:T(8,128)} fusion(f32[2,5184,72]{2,1,0:T(8,128)} %reshape.315, s32[72]{0:T(128)S(1)} %add_select_fusion.1, pred[72]{0:T(512)(128)(4,1)S(1)} %iota_compare_fusion), kind=kOutput, calls=%fused_computation.11 | convolution fusion | flops 645024384 | bytes 5972328 | tf_op jit(solution)/shard_map/pmk,kr->prm/dot_general | solution.py:51
  282.2 10.3 %convolution_bitcast_fusion.4 = f32[2,72,5184]{2,1,0:T(8,128)} fusion(f32[2,5184,72]{2,1,0:T(8,128)} %broadcast_in_dim_reshape.2, f32[5184,72]{1,0:T(8,128)} %mul.401, s32[72]{0:T(128)S(1)} %add_select_fusion.1, pred[72]{0:T(512)(128)(4,1)S(1)} %iota_compare_fusion), kind=kOutput, calls=%fused_computation.10 | convolution fusion | flops 645770880 | bytes 7465320 | tf_op jit(solution)/shard_map/pmc,kc->pkm/dot_general | solution.py:47
  298.3 9.3 %convolution_bitcast_fusion.3 = f32[2,72,5184]{2,1,0:T(8,128)} fusion(f32[2,5184,72]{2,1,0:T(8,128)} %reshape.316, s32[72]{0:T(128)S(1)} %add_select_fusion.1, pred[72]{0:T(512)(128)(4,1)S(1)} %iota_compare_fusion), kind=kOutput, calls=%fused_computation.9 | convolution fusion | flops 645024384 | bytes 5972328 | tf_op jit(solution)/shard_map/pmc,kc->pkm/dot_general | solution.py:47
  313.7 9.8 %fusion.2 = f32[2,72,5184]{2,1,0:T(8,128)} fusion(f32[2,5184,72]{2,1,0:T(8,128)} %reshape.317, f32[72,5184]{1,0:T(8,128)} %fusion.11, s32[72]{0:T(128)S(1)} %add_select_fusion.1, pred[72]{0:T(512)(128)(4,1)S(1)} %iota_compare_fusion), kind=kOutput, calls=%fused_computation.5 | convolution fusion | flops 645770880 | bytes 7465320 | tf_op jit(solution)/shard_map/pmc,kc->pkm/dot_general | solution.py:47
  329.3 9.6 %convolution_bitcast_fusion.2 = f32[2,72,5184]{2,1,0:T(8,128)} fusion(f32[2,5184,72]{2,1,0:T(8,128)} %reshape.318, s32[72]{0:T(128)S(1)} %add_select_fusion.1, pred[72]{0:T(512)(128)(4,1)S(1)} %iota_compare_fusion), kind=kOutput, calls=%fused_computation.8 | convolution fusion | flops 645024384 | bytes 5972328 | tf_op jit(solution)/shard_map/pmk,kr->prm/dot_general | solution.py:51
  344.7 9.6 %convolution_bitcast_fusion.1 = f32[2,72,5184]{2,1,0:T(8,128)} fusion(f32[2,5184,72]{2,1,0:T(8,128)} %reshape.319, s32[72]{0:T(128)S(1)} %add_select_fusion.1, pred[72]{0:T(512)(128)(4,1)S(1)} %iota_compare_fusion), kind=kOutput, calls=%fused_computation.7 | convolution fusion | flops 645024384 | bytes 5972328 | tf_op jit(solution)/shard_map/pmk,kr->prm/dot_general | solution.py:51
  362.7 12.0 %multiply_reduce_fusion = (f32[72,5184]{1,0:T(8,128)S(1)}, f32[72,5184]{1,0:T(8,128)S(1)}, f32[72,5184]{1,0:T(8,128)S(1)}, f32[2,72,5184]{2,1,0:T(8,128)S(1)}) fusion(f32[2,72,5184]{2,0,1:T(2,128)S(1)} %bitcast.123, f32[2,72,5184]{2,1,0:T(8,128)} %convolution_bitcast_fusion.5, f32[2,72,5184]{2,1,0:T(8,128)S(1)} %copy-done, f32[72,5184]{1,0:T(8,128)S(1)} %bitcast.127, ...), kind=kOutput, calls=%fused_computation.25 | convolution fusion | flops 654355584 | bytes 23888232 | tf_op jit(solution)/shard_map/pmk,kr->prm/dot_general | solution.py:51
  377.9 17.7 %collective-permute-done.3 = f32[1,72,5184]{2,1,0:T(8,128)S(1)} collective-permute-done((f32[1,72,5184]{2,1,0:T(8,128)S(1)}, f32[1,72,5184]{2,1,0:T(8,128)S(1)}, u32[]{:S(2)}, u32[]{:S(2)}) %collective-permute-start.3) | collective-permute-done | bytes 1493024 | tf_op jit(solution)/shard_map/ppermute | solution.py:15
  395.8 20.7 %collective-permute-done.4 = f32[1,72,5184]{2,1,0:T(8,128)S(1)} collective-permute-done((f32[1,72,5184]{2,1,0:T(8,128)S(1)}, f32[1,72,5184]{2,1,0:T(8,128)S(1)}, u32[]{:S(2)}, u32[]{:S(2)}) %collective-permute-start.4) | collective-permute-done | bytes 1493024 | tf_op jit(solution)/shard_map/ppermute | solution.py:15
  416.7 6.7 %collective-permute-start.5 = (f32[1,72,5184]{2,1,0:T(8,128)S(1)}, f32[1,72,5184]{2,1,0:T(8,128)S(1)}, u32[]{:S(2)}, u32[]{:S(2)}) collective-permute-start(f32[1,72,5184]{2,1,0:T(8,128)S(1)} %bitcast_add_fusion), channel_id=1, source_target_pairs={{0,122},{2,124},{4,126},{6,0},{8,2},{10,4},{12,6},{14,8},{16,10},{... | collective-permute-start | bytes 4478984 | tf_op jit(solution)/shard_map/ppermute | solution.py:15
  423.4 33.5 %collective-permute-done.5 = f32[1,72,5184]{2,1,0:T(8,128)S(1)} collective-permute-done((f32[1,72,5184]{2,1,0:T(8,128)S(1)}, f32[1,72,5184]{2,1,0:T(8,128)S(1)}, u32[]{:S(2)}, u32[]{:S(2)}) %collective-permute-start.5) | collective-permute-done | bytes 1493024 | tf_op jit(solution)/shard_map/ppermute | solution.py:15
  458.8 34.3 %all_to_all.10 = f32[2,2,36,5184]{3,1,2,0:T(2,128)} all-to-all(f32[2,2,36,5184]{3,1,2,0:T(2,128)S(1)} %bitcast.124), channel_id=1, replica_groups=mesh['band'=64,'grid'=2] {'grid'}, dimensions={0} | all-to-all | bytes 5971968 | tf_op jit(solution)/shard_map/all_to_all | solution.py:25
  (60 shorter events, 172.6 us)
Async XLA Ops:
  4.9 38.9 %all-to-all-start = ((f32[2,2,36,5184]{3,1,2,0:T(2,128)}), f32[2,2,36,5184]{3,1,2,0:T(2,128)S(1)}, u32[]{:S(2)}, u32[]{:S(2)}) async-start(f32[2,2,36,5184]{3,1,2,0:T(2,128)} %pad_maximum_fusion), calls=%async_computation | async-start | bytes 6045696 | tf_op jit(solution)/shard_map/all_to_all | solution.py:83
  46.3 22.0 %collective-permute-start = (f32[1,72,5184]{2,0,1:T(1,128)}, f32[1,72,5184]{2,0,1:T(1,128)}, u32[]{:S(2)}, u32[]{:S(2)}) collective-permute-start(f32[1,72,5184]{2,0,1:T(1,128)} %constant_dynamic-slice_fusion), channel_id=1, source_target_pairs={{0,2},{2,4},{4,6},{6,8},{8,10},{10,12},{12,14},{14,16},{16,18},{18... | collective-permute-start | bytes 4478984 | tf_op jit(solution)/shard_map/ppermute | solution.py:15
  109.8 61.8 %collective-permute-start.1 = (f32[1,72,5184]{2,0,1:T(1,128)}, f32[1,72,5184]{2,0,1:T(1,128)}, u32[]{:S(2)}, u32[]{:S(2)}) collective-permute-start(f32[1,72,5184]{2,0,1:T(1,128)} %collective-permute-done), channel_id=1, source_target_pairs={{0,2},{2,4},{4,6},{6,8},{8,10},{10,12},{12,14},{14,16},{16,18},{18... | collective-permute-start | bytes 4478984 | tf_op jit(solution)/shard_map/ppermute | solution.py:15
  212.7 59.5 %collective-permute-start.2 = (f32[1,72,5184]{2,0,1:T(1,128)}, f32[1,72,5184]{2,0,1:T(1,128)}, u32[]{:S(2)}, u32[]{:S(2)}) collective-permute-start(f32[1,72,5184]{2,0,1:T(1,128)} %collective-permute-done.1), channel_id=1, source_target_pairs={{0,2},{2,4},{4,6},{6,8},{8,10},{10,12},{12,14},{14,16},{16,18},{18... | collective-permute-start | bytes 4478984 | tf_op jit(solution)/shard_map/ppermute | solution.py:15
  360.4 2.3 copy-start
  374.8 20.8 %collective-permute-start.3 = (f32[1,72,5184]{2,1,0:T(8,128)S(1)}, f32[1,72,5184]{2,1,0:T(8,128)S(1)}, u32[]{:S(2)}, u32[]{:S(2)}) collective-permute-start(f32[1,72,5184]{2,1,0:T(8,128)S(1)} %negate_bitcast_fusion), channel_id=1, source_target_pairs={{0,2},{2,4},{4,6},{6,8},{8,10},{10,12},{12,14},{14,16},{16,18},{18... | collective-permute-start | bytes 4478984 | tf_op jit(solution)/shard_map/ppermute | solution.py:15
  395.7 20.8 %collective-permute-start.4 = (f32[1,72,5184]{2,1,0:T(8,128)S(1)}, f32[1,72,5184]{2,1,0:T(8,128)S(1)}, u32[]{:S(2)}, u32[]{:S(2)}) collective-permute-start(f32[1,72,5184]{2,1,0:T(8,128)S(1)} %bitcast_add_fusion.1), channel_id=1, source_target_pairs={{0,2},{2,4},{4,6},{6,8},{8,10},{10,12},{12,14},{14,16},{16,18},{18... | collective-permute-start | bytes 4478984 | tf_op jit(solution)/shard_map/ppermute | solution.py:15
  416.7 40.2 %collective-permute-start.5 = (f32[1,72,5184]{2,1,0:T(8,128)S(1)}, f32[1,72,5184]{2,1,0:T(8,128)S(1)}, u32[]{:S(2)}, u32[]{:S(2)}) collective-permute-start(f32[1,72,5184]{2,1,0:T(8,128)S(1)} %bitcast_add_fusion), channel_id=1, source_target_pairs={{0,122},{2,124},{4,126},{6,0},{8,2},{10,4},{12,6},{14,8},{16,10},{... | collective-permute-start | bytes 4478984 | tf_op jit(solution)/shard_map/ppermute | solution.py:15
